TPU v7x, 32 devices: a whole 2x2x4 slice. The times are simulated.
32 devices in a mesh: grp: 4 (over y, core), loc: 8 (over z, x).
Axes of the slice: x: 2, y: 2, z: 4, core: 2. Of those that a mesh axis runs over, the one named last changes fastest.
Arguments:
- tokens: bfloat16 [8192, 1024], P(('grp', 'loc')), may hold values from -6 to 6
- w_gate: bfloat16 [32, 1024, 2816], P(('grp', 'loc')), may hold values from -0.1875 to 0.1875
- w_up: bfloat16 [32, 1024, 2816], P(('grp', 'loc')), may hold values from -0.1875 to 0.1875
- w_down: bfloat16 [32, 2816, 1024], P(('grp', 'loc')), may hold values from -0.109375 to 0.109375
- chosen: int32 [32, 128], replicated, may hold values from -1 to 8191, as said below
- gate_weights: float32 [32, 128], replicated, may hold values from 0.05 to 1
Outputs:
- combined: bfloat16 [8192, 1024], P(('grp', 'loc'))
Inputs may be any that keep to these rules, and one draw needn't show every extreme that they name: `chosen`: each entry is a token index or -1 for an empty slot, empty slots anywhere in a row. One expert's row names a token at most once. At most 8 entries of one expert's row lie among the 256 tokens of one device, and every expert has exactly 8 from some device. Some expert has no empty slot.
All inputs are finite; a program needn't handle non-finite values.
Results may differ from a plain program's by a relative error of at most 0.0085.
Values may be sent and summed in bfloat16 or wider, within the bound.
A program may use at most 128 MiB of HBM per device.

v0:
```python
import functools

import jax
import jax.numpy as jnp
from jax import lax
from jax.experimental import pallas as pl
from jax.experimental.pallas import tpu as pltpu
from jax.sharding import PartitionSpec as P

PAIR_MOST = 8
WIDE = 256
WEIGHT_CUTS = 4
MESH = pl.DeviceIdType.MESH
F32 = jnp.float32
BF16 = jnp.bfloat16


def plan(local_count):
    half = local_count // 2
    far_even = [(1, j) for j in range(0, half, 2)]
    far_odd = [(1, j) for j in range(1, half, 2)]
    near = [(0, j) for j in range(half)]
    if half % 2:
        return [far_even + far_odd + near]
    return [far_even + near, far_odd]


def tile_of(size):
    for tile in (WIDE, 128):
        if size % tile == 0:
            return tile
    return size


def kernel(
    passes,
    tokens_hbm,
    gate_hbm,
    up_hbm,
    down_hbm,
    chosen_hbm,
    weight_hbm,
    out_ref,
    tokens,
    w_gate,
    w_up,
    w_down,
    chosen,
    weights,
    chosen_rows,
    weight_rows,
    outgoing,
    received,
    produced,
    back,
    gathered,
    hidden,
    total,
    *rest,
):
    mix_hi, mix_lo = rest[: len(passes)], rest[len(passes) : 2 * len(passes)]
    small_sem, load_sem, send_sem, recv_sem, return_send_sem, return_sem = rest[2 * len(passes) :]
    group_count, local_count = lax.axis_size("grp"), lax.axis_size("loc")
    devices = group_count * local_count
    half = local_count // 2
    grp, loc = lax.axis_index("grp"), lax.axis_index("loc")
    me = grp * local_count + loc
    side, spot = loc // half, loc % half
    groups = [group for one in passes for group in one]

    blocks = []
    starts = [0]
    for number, one in enumerate(passes):
        for flip, step in one:
            for turn in range(group_count):
                peer_grp = lax.rem(grp + turn, group_count)
                peer_loc = lax.rem(side + flip, 2) * half + lax.rem(spot + step, half)
                mirror = groups.index((flip, (half - step) % half)) * group_count
                mirror += (group_count - turn) % group_count
                own = flip == 0 and step == 0 and turn == 0
                blocks.append((number, peer_grp, peer_loc, mirror, own))
        starts.append(len(blocks))

    barrier = pltpu.get_barrier_semaphore()

    def greet(turn, carry):
        peer = lax.rem(me + turn, devices)
        pl.semaphore_signal(
            barrier, inc=1, device_id=(peer // local_count, peer % local_count), device_id_type=MESH
        )
        return carry

    lax.fori_loop(1, devices, greet, 0)

    small = [
        pltpu.make_async_copy(chosen_hbm, chosen, small_sem.at[0]),
        pltpu.make_async_copy(weight_hbm, weights, small_sem.at[1]),
        pltpu.make_async_copy(tokens_hbm, tokens, small_sem.at[2]),
    ]
    for copy in small:
        copy.start()
    loads = []
    for number, (source, place) in enumerate(
        ((gate_hbm, w_gate), (up_hbm, w_up), (down_hbm, w_down))
    ):
        depth = place.shape[0] // WEIGHT_CUTS
        for cut in range(WEIGHT_CUTS):
            rows = pl.ds(cut * depth, depth)
            copy = pltpu.make_async_copy(
                source.at[0, rows], place.at[rows], load_sem.at[number * WEIGHT_CUTS + cut]
            )
            copy.start()
            loads.append(copy)

    small[0].wait()
    small[1].wait()
    slot_total = chosen.shape[1]
    for at, (_, peer_grp, peer_loc, _, _) in enumerate(blocks):
        expert = peer_grp * local_count + peer_loc
        rows = pl.ds(at * PAIR_MOST, PAIR_MOST)
        chosen_rows[rows, :] = jnp.broadcast_to(
            chosen[pl.ds(expert, 1), :], (PAIR_MOST, slot_total)
        )
        weight_rows[rows, :] = jnp.broadcast_to(
            weights[pl.ds(expert, 1), :], (PAIR_MOST, slot_total)
        )
    token_count, width = tokens.shape
    row_total = devices * PAIR_MOST
    local = chosen_rows[...] - me * token_count
    mine = (local >= 0) & (local < token_count)
    earlier = lax.broadcasted_iota(jnp.int32, (slot_total, slot_total), 0)
    later = lax.broadcasted_iota(jnp.int32, (slot_total, slot_total), 1)
    before = jnp.where(earlier < later, 1.0, 0.0).astype(BF16)
    rank = jnp.dot(
        jnp.where(mine, 1.0, 0.0).astype(BF16), before, preferred_element_type=F32
    )
    wanted = lax.broadcasted_iota(jnp.int32, (row_total, slot_total), 0) % PAIR_MOST
    hit = mine & (rank == wanted.astype(F32))
    pick = jnp.sum(jnp.where(hit, local.astype(F32) + 1.0, 0.0), axis=1, keepdims=True) - 1.0
    pick_weight = jnp.sum(jnp.where(hit, weight_rows[...], 0.0), axis=1, keepdims=True)
    token_iota = lax.broadcasted_iota(jnp.int32, (row_total, token_count), 1).astype(F32)
    select = pick == token_iota
    select_table = jnp.where(select, 1.0, 0.0).astype(BF16)
    small[2].wait()
    picked = jnp.dot(select_table, tokens[...], preferred_element_type=F32)
    outgoing[...] = picked.reshape(devices, PAIR_MOST, width).astype(BF16)

    pl.semaphore_wait(barrier, devices - 1)

    def send(source, place, send_sems, recv_sems, at):
        number, peer_grp, peer_loc, mirror, own = blocks[at]
        if own:
            pltpu.make_async_copy(source.at[at], place.at[mirror], recv_sems.at[number]).start()
        else:
            pltpu.make_async_remote_copy(
                src_ref=source.at[at],
                dst_ref=place.at[mirror],
                send_sem=send_sems.at[0],
                recv_sem=recv_sems.at[number],
                device_id=(peer_grp, peer_loc),
                device_id_type=MESH,
            ).start()

    def wait_blocks(place, sem, first, count):
        view = place.at[pl.ds(first, count)]
        pltpu.make_async_copy(view, view, sem).wait()

    for at in range(devices):
        send(outgoing, received, send_sem, recv_sem, at)

    mixing = jnp.where(select, pick_weight, 0.0)
    for number in range(len(passes)):
        first, last = starts[number] * PAIR_MOST, starts[number + 1] * PAIR_MOST
        turned = mixing[first:last].T
        high = turned.astype(BF16)
        mix_hi[number][...] = high
        mix_lo[number][...] = (turned - high.astype(F32)).astype(BF16)

    for copy in loads:
        copy.wait()

    hidden_total = w_gate.shape[1]
    hidden_tile, width_tile = tile_of(hidden_total), tile_of(width)
    for number in range(len(passes)):
        first, count = starts[number], starts[number + 1] - starts[number]
        rows = count * PAIR_MOST
        wait_blocks(received, recv_sem.at[number], first, count)
        arrived = received[pl.ds(first, count)].astype(F32)
        gathered[:rows, :] = arrived.reshape(rows, width).astype(BF16)

        def expand(tile, carry, rows=rows):
            columns = pl.ds(pl.multiple_of(tile * hidden_tile, hidden_tile), hidden_tile)
            gate_pre = jnp.dot(gathered[:rows, :], w_gate[:, columns], preferred_element_type=F32)
            up_pre = jnp.dot(gathered[:rows, :], w_up[:, columns], preferred_element_type=F32)
            hidden[:rows, columns] = (gate_pre / (1.0 + jnp.exp(-gate_pre)) * up_pre).astype(BF16)
            return carry

        lax.fori_loop(0, hidden_total // hidden_tile, expand, 0, unroll=True)

        def contract(tile, carry, rows=rows, first=first, count=count):
            columns = pl.ds(pl.multiple_of(tile * width_tile, width_tile), width_tile)
            result = jnp.dot(hidden[:rows, :], w_down[:, columns], preferred_element_type=F32)
            produced[pl.ds(first, count), :, columns] = result.reshape(
                count, PAIR_MOST, width_tile
            ).astype(BF16)
            return carry

        lax.fori_loop(0, width // width_tile, contract, 0, unroll=True)
        for at in range(first, first + count):
            send(produced, back, return_send_sem, return_sem, at)

    for number in range(len(passes)):
        first, count = starts[number], starts[number + 1] - starts[number]
        rows = count * PAIR_MOST
        wait_blocks(back, return_sem.at[number], first, count)
        returned = back[pl.ds(first, count)].astype(F32).reshape(rows, width).astype(BF16)
        part = jnp.dot(mix_hi[number][...], returned, preferred_element_type=F32)
        part += jnp.dot(mix_lo[number][...], returned, preferred_element_type=F32)
        if number:
            part += total[...]
        if number == len(passes) - 1:
            out_ref[...] = part.astype(out_ref.dtype)
        else:
            total[...] = part
    wait_blocks(outgoing, send_sem.at[0], 0, devices - 1)
    wait_blocks(produced, return_send_sem.at[0], 0, devices - 1)


def shards(tokens, w_gate, w_up, w_down, chosen, gate_weights):
    local_count = lax.axis_size("loc")
    devices = lax.axis_size("grp") * local_count
    passes = plan(local_count)
    token_count, width = tokens.shape
    hidden_total = w_gate.shape[2]
    row_total = devices * PAIR_MOST
    pass_rows = [len(one) * lax.axis_size("grp") * PAIR_MOST for one in passes]
    table = pltpu.VMEM((devices, PAIR_MOST, width), BF16)
    anywhere = pl.BlockSpec(memory_space=pl.ANY)
    return pl.pallas_call(
        functools.partial(kernel, passes),
        out_shape=pltpu.VMEM((token_count, width), BF16),
        in_specs=[anywhere] * 6,
        out_specs=pl.BlockSpec(memory_space=pltpu.VMEM),
        scratch_shapes=[
            pltpu.VMEM((token_count, width), BF16),
            pltpu.VMEM(w_gate.shape[1:], BF16),
            pltpu.VMEM(w_up.shape[1:], BF16),
            pltpu.VMEM(w_down.shape[1:], BF16),
            pltpu.VMEM(chosen.shape, jnp.int32),
            pltpu.VMEM(chosen.shape, F32),
            pltpu.VMEM((row_total, chosen.shape[1]), jnp.int32),
            pltpu.VMEM((row_total, chosen.shape[1]), F32),
            table,
            table,
            table,
            table,
            pltpu.VMEM((max(pass_rows), width), BF16),
            pltpu.VMEM((max(pass_rows), hidden_total), BF16),
            pltpu.VMEM((token_count, width), F32),
            *[pltpu.VMEM((token_count, rows), BF16) for rows in pass_rows],
            *[pltpu.VMEM((token_count, rows), BF16) for rows in pass_rows],
            pltpu.SemaphoreType.DMA((3,)),
            pltpu.SemaphoreType.DMA((3 * WEIGHT_CUTS,)),
            pltpu.SemaphoreType.DMA((1,)),
            pltpu.SemaphoreType.DMA((len(passes),)),
            pltpu.SemaphoreType.DMA((1,)),
            pltpu.SemaphoreType.DMA((len(passes),)),
        ],
        compiler_params=pltpu.CompilerParams(
            collective_id=0, has_side_effects=True, vmem_limit_bytes=58 * 1024 * 1024
        ),
    )(tokens, w_gate, w_up, w_down, chosen, gate_weights)


def solution(mesh):
    return jax.shard_map(
        shards,
        mesh=mesh,
        in_specs=(
            P(("grp", "loc"), None),
            P(("grp", "loc"), None, None),
            P(("grp", "loc"), None, None),
            P(("grp", "loc"), None, None),
            P(),
            P(),
        ),
        out_specs=P(("grp", "loc"), None),
        check_vma=False,
    )
```

profile of v0, /device:TPU:0, one launch (start us, length us, event | category | flops | bytes accessed | tf_op | source)
XLA Modules:
  0.0 38.1 jit_solution(7995434467081773615)
XLA Ops:
  0.0 37.2 %shard_map.64 = bf16[256,1024]{1,0:T(8,128)(2,1)S(1)} custom-call(bf16[256,1024]{1,0:T(8,128)(2,1)} %tokens_hbm.1, bf16[1,1024,2816]{2,1,0:T(8,128)(2,1)} %gate_hbm.1, bf16[1,1024,2816]{2,1,0:T(8,128)(2,1)} %up_hbm.1, bf16[1,2816,1024]{2,1,0:T(8,128)(2,1)} %down_hbm.1, s32[32,128]{1,0:T(8,128)} %chosen_hbm.1, f32[32,128]{1,0:T(8,128)} %weight_hbm.1), custom_call_target="tpu_custom_call" | custom-call | tf_op jit(solution)/shard_map/pallas_call | solution.py:239
  37.3 0.8 %copy.8 = bf16[256,1024]{1,0:T(8,128)(2,1)} copy(bf16[256,1024]{1,0:T(8,128)(2,1)S(1)} %shard_map.64) | data formatting | bytes 1048576
where the time goes:
time: 38.2 us; the launch traced here: 38.1 us
  Pallas kernels  37.2 us (97%)
  local copies, waits for them, and re-layouts  0.8 us (2%)
    pallas_call x1, Pallas kernels, shards(): pl.pallas_call(functools.partial(kernel, passes), out_shape=pltpu.VMEM((t...  37.2 us
    unnamed x1, local copies, waits for them, and re-layouts  0.8 us

commit v1 on v0

--- a/solution.py
+++ b/solution.py
@@ -99,19 +99,6 @@
     ]
     for copy in small:
         copy.start()
-    loads = []
-    for number, (source, place) in enumerate(
-        ((gate_hbm, w_gate), (up_hbm, w_up), (down_hbm, w_down))
-    ):
-        depth = place.shape[0] // WEIGHT_CUTS
-        for cut in range(WEIGHT_CUTS):
-            rows = pl.ds(cut * depth, depth)
-            copy = pltpu.make_async_copy(
-                source.at[0, rows], place.at[rows], load_sem.at[number * WEIGHT_CUTS + cut]
-            )
-            copy.start()
-            loads.append(copy)
-
     small[0].wait()
     small[1].wait()
     slot_total = chosen.shape[1]
@@ -142,6 +129,19 @@
     select = pick == token_iota
     select_table = jnp.where(select, 1.0, 0.0).astype(BF16)
     small[2].wait()
+    loads = []
+    for number, (source, place) in enumerate(
+        ((gate_hbm, w_gate), (up_hbm, w_up), (down_hbm, w_down))
+    ):
+        depth = place.shape[0] // WEIGHT_CUTS
+        for cut in range(WEIGHT_CUTS):
+            rows = pl.ds(cut * depth, depth)
+            copy = pltpu.make_async_copy(
+                source.at[0, rows], place.at[rows], load_sem.at[number * WEIGHT_CUTS + cut]
+            )
+            copy.start()
+            loads.append(copy)
+
     picked = jnp.dot(select_table, tokens[...], preferred_element_type=F32)
     outgoing[...] = picked.reshape(devices, PAIR_MOST, width).astype(BF16)
 

time: 38.2 us -> 34.7 us (0.908)
  Pallas kernels: 37.2 us -> 33.7 us
    pallas_call x1, Pallas kernels: 37.2 us -> 33.7 us  [shards(): pl.pallas_call(functools.partial(kernel, passes), out_shape=pltpu.VMEM((t...]
where the time goes in v1:
time: 34.7 us; the launch traced here: 34.5 us
  Pallas kernels  33.7 us (97%)
  local copies, waits for them, and re-layouts  0.8 us (2%)
    pallas_call x1, Pallas kernels, shards(): pl.pallas_call(functools.partial(kernel, passes), out_shape=pltpu.VMEM((t...  33.7 us
    unnamed x1, local copies, waits for them, and re-layouts  0.8 us

profile of v1, /device:TPU:0, one launch (start us, length us, event | category | flops | bytes accessed | tf_op | source)
XLA Modules:
  0.0 34.5 jit_solution(3664823615637261738)
XLA Ops:
  0.0 33.7 %shard_map.64 = bf16[256,1024]{1,0:T(8,128)(2,1)S(1)} custom-call(bf16[256,1024]{1,0:T(8,128)(2,1)} %tokens_hbm.1, bf16[1,1024,2816]{2,1,0:T(8,128)(2,1)} %gate_hbm.1, bf16[1,1024,2816]{2,1,0:T(8,128)(2,1)} %up_hbm.1, bf16[1,2816,1024]{2,1,0:T(8,128)(2,1)} %down_hbm.1, s32[32,128]{1,0:T(8,128)} %chosen_hbm.1, f32[32,128]{1,0:T(8,128)} %weight_hbm.1), custom_call_target="tpu_custom_call" | custom-call | tf_op jit(solution)/shard_map/pallas_call | solution.py:239
  33.7 0.8 %copy.8 = bf16[256,1024]{1,0:T(8,128)(2,1)} copy(bf16[256,1024]{1,0:T(8,128)(2,1)S(1)} %shard_map.64) | data formatting | bytes 1048576

commit v2 on v1

v2 whole, which is shorter than its diff:
```python
import jax
import jax.numpy as jnp
from jax import lax
from jax.experimental import pallas as pl
from jax.experimental.pallas import tpu as pltpu
from jax.sharding import PartitionSpec as P

PAIR_MOST = 8
WIDE = 256
WEIGHT_CUTS = 4
MESH = pl.DeviceIdType.MESH
F32 = jnp.float32
BF16 = jnp.bfloat16


def tile_of(size):
    for tile in (WIDE, 128):
        if size % tile == 0:
            return tile
    return size


def flip(value, mask):
    bit = 1
    while bit <= mask:
        if mask & bit:
            value = value + bit - 2 * bit * (value // bit % 2)
        bit *= 2
    return value


def kernel(
    tokens_hbm,
    gate_hbm,
    up_hbm,
    down_hbm,
    chosen_hbm,
    weight_hbm,
    out_ref,
    tokens,
    w_gate,
    w_up,
    w_down,
    chosen,
    weights,
    chosen_rows,
    weight_rows,
    outgoing,
    received,
    produced,
    back,
    gathered,
    hidden,
    total,
    mix_hi,
    mix_lo,
    small_sem,
    load_sem,
    send_sem,
    recv_sem,
    return_send_sem,
    return_sem,
):
    group_count, local_count = lax.axis_size("grp"), lax.axis_size("loc")
    devices = group_count * local_count
    quarter = local_count // 4
    grp, loc = lax.axis_index("grp"), lax.axis_index("loc")
    me = grp * local_count + loc
    plane, spot = loc // quarter, loc % quarter
    side = plane // 2
    outer = (side + plane % 2 + 1) % 2
    block = quarter * group_count
    part = block // 2

    def partner(plane_there, turn):
        return (
            flip(grp, turn % group_count),
            plane_there * quarter + flip(spot, turn // group_count),
        )

    def far_plane(kind):
        return side * (1 - kind) + (1 - side) * (2 + kind)

    def near_out(other, turn):
        return other * block + turn

    def far_out(sub, kind, turn):
        return (2 + sub) * block + kind * part + turn

    def near_in(other, turn):
        return other * (block + part) + turn

    def far_in(sub, kind, turn):
        return turn + (7 * part - kind * part if sub else block + kind * (block + part))

    def far_pass(sub, kind):
        return 3 - kind if sub else kind

    dispatch, results = [], [[], [], [], []]
    for sub in range(2):
        for turn in range(part):
            for kind in range(2):
                peer = partner(far_plane(kind), sub * part + turn)
                there, number = far_in(sub, outer, turn), far_pass(sub, outer)
                dispatch.append((far_out(sub, kind, turn), peer, there, number))
                home = far_out(sub, outer, turn)
                results[far_pass(sub, kind)].append((far_in(sub, kind, turn), peer, home, 1 + sub))
    near = []
    for other in (1, 0):
        for turn in range(block):
            peer = partner(flip(plane, other), turn)
            near.append((near_out(other, turn), peer, near_in(other, turn), other))
            results[other].append((near_in(other, turn), peer, near_out(other, turn), 0))
    dispatch = near + dispatch
    passes = [
        (0, block + part), (block + part, block + part), (6 * part, part), (7 * part, part)
    ]
    groups = [(0, 2 * block), (2 * block, block), (3 * block, block)]
    barrier = pltpu.get_barrier_semaphore()
    for at, peer, _, _ in reversed(dispatch):
        if at:
            pl.semaphore_signal(barrier, inc=1, device_id=peer, device_id_type=MESH)
    small = [
        pltpu.make_async_copy(chosen_hbm, chosen, small_sem.at[0]),
        pltpu.make_async_copy(weight_hbm, weights, small_sem.at[1]),
        pltpu.make_async_copy(tokens_hbm, tokens, small_sem.at[2]),
    ]
    for copy in small:
        copy.start()

    small[0].wait()
    small[1].wait()
    slot_total = chosen.shape[1]
    for at, (peer_grp, peer_loc), _, _ in dispatch:
        expert = peer_grp * local_count + peer_loc
        rows = pl.ds(at * PAIR_MOST, PAIR_MOST)
        chosen_rows[rows, :] = jnp.broadcast_to(
            chosen[pl.ds(expert, 1), :], (PAIR_MOST, slot_total)
        )
        weight_rows[rows, :] = jnp.broadcast_to(
            weights[pl.ds(expert, 1), :], (PAIR_MOST, slot_total)
        )
    token_count, width = tokens.shape
    row_total = devices * PAIR_MOST
    local = chosen_rows[...] - me * token_count
    mine = (local >= 0) & (local < token_count)
    earlier = lax.broadcasted_iota(jnp.int32, (slot_total, slot_total), 0)
    later = lax.broadcasted_iota(jnp.int32, (slot_total, slot_total), 1)
    before = jnp.where(earlier < later, 1.0, 0.0).astype(BF16)
    rank = jnp.dot(
        jnp.where(mine, 1.0, 0.0).astype(BF16), before, preferred_element_type=F32
    )
    wanted = lax.broadcasted_iota(jnp.int32, (row_total, slot_total), 0) % PAIR_MOST
    hit = mine & (rank == wanted.astype(F32))
    pick = jnp.sum(jnp.where(hit, local.astype(F32) + 1.0, 0.0), axis=1, keepdims=True) - 1.0
    pick_weight = jnp.sum(jnp.where(hit, weight_rows[...], 0.0), axis=1, keepdims=True)
    token_iota = lax.broadcasted_iota(jnp.int32, (row_total, token_count), 1).astype(F32)
    select = pick == token_iota
    select_table = jnp.where(select, 1.0, 0.0).astype(BF16)
    small[2].wait()
    loads = []
    for number, (source, place) in enumerate(
        ((gate_hbm, w_gate), (up_hbm, w_up), (down_hbm, w_down))
    ):
        depth = place.shape[0] // WEIGHT_CUTS
        for cut in range(WEIGHT_CUTS):
            rows = pl.ds(cut * depth, depth)
            copy = pltpu.make_async_copy(
                source.at[0, rows], place.at[rows], load_sem.at[number * WEIGHT_CUTS + cut]
            )
            copy.start()
            loads.append(copy)
    picked = jnp.dot(select_table, tokens[...], preferred_element_type=F32)
    outgoing[...] = picked.reshape(devices, PAIR_MOST, width).astype(BF16)
    pl.semaphore_wait(barrier, devices - 1)

    def send(source, place, send_sems, sems, entry):
        at, peer, mirror, sem = entry
        if at:
            pltpu.make_async_remote_copy(
                src_ref=source.at[at],
                dst_ref=place.at[mirror],
                send_sem=send_sems.at[0],
                recv_sem=sems.at[sem],
                device_id=peer,
                device_id_type=MESH,
            ).start()
        else:
            pltpu.make_async_copy(source.at[at], place.at[mirror], sems.at[sem]).start()

    def wait_blocks(place, sem, first, count):
        view = place.at[pl.ds(first, count)]
        pltpu.make_async_copy(view, view, sem).wait()

    for entry in dispatch:
        send(outgoing, received, send_sem, recv_sem, entry)
    mixing = jnp.where(select, pick_weight, 0.0).T
    high = mixing.astype(BF16)
    low = (mixing - high.astype(F32)).astype(BF16)
    for number, (first, count) in enumerate(groups):
        rows = slice(first * PAIR_MOST, (first + count) * PAIR_MOST)
        mix_hi[number][...] = high[:, rows]
        mix_lo[number][...] = low[:, rows]
    for copy in loads:
        copy.wait()

    hidden_total = w_gate.shape[1]
    hidden_tile, width_tile = tile_of(hidden_total), tile_of(width)
    for number, (first, count) in enumerate(passes):
        rows = count * PAIR_MOST
        wait_blocks(received, recv_sem.at[number], first, count)
        arrived = received[pl.ds(first, count)].astype(F32)
        gathered[:rows, :] = arrived.reshape(rows, width).astype(BF16)

        def expand(tile, carry, rows=rows):
            columns = pl.ds(pl.multiple_of(tile * hidden_tile, hidden_tile), hidden_tile)
            gate_pre = jnp.dot(gathered[:rows, :], w_gate[:, columns], preferred_element_type=F32)
            up_pre = jnp.dot(gathered[:rows, :], w_up[:, columns], preferred_element_type=F32)
            hidden[:rows, columns] = (gate_pre / (1.0 + jnp.exp(-gate_pre)) * up_pre).astype(BF16)
            return carry

        lax.fori_loop(0, hidden_total // hidden_tile, expand, 0, unroll=True)

        def contract(tile, carry, rows=rows, first=first, count=count):
            columns = pl.ds(pl.multiple_of(tile * width_tile, width_tile), width_tile)
            result = jnp.dot(hidden[:rows, :], w_down[:, columns], preferred_element_type=F32)
            produced[pl.ds(first, count), :, columns] = result.reshape(
                count, PAIR_MOST, width_tile
            ).astype(BF16)
            return carry

        lax.fori_loop(0, width // width_tile, contract, 0, unroll=True)
        for entry in results[number]:
            send(produced, back, return_send_sem, return_sem, entry)

    for number, (first, count) in enumerate(groups):
        rows = count * PAIR_MOST
        wait_blocks(back, return_sem.at[number], first, count)
        returned = back[pl.ds(first, count)].astype(F32).reshape(rows, width).astype(BF16)
        result = jnp.dot(mix_hi[number][...], returned, preferred_element_type=F32)
        result += jnp.dot(mix_lo[number][...], returned, preferred_element_type=F32)
        if number:
            result += total[...]
        if number == len(groups) - 1:
            out_ref[...] = result.astype(out_ref.dtype)
        else:
            total[...] = result
    wait_blocks(outgoing, send_sem.at[0], 0, devices - 1)
    wait_blocks(produced, return_send_sem.at[0], 0, devices - 1)


def shards(tokens, w_gate, w_up, w_down, chosen, gate_weights):
    local_count = lax.axis_size("loc")
    devices = lax.axis_size("grp") * local_count
    token_count, width = tokens.shape
    hidden_total = w_gate.shape[2]
    row_total = devices * PAIR_MOST
    pass_rows = row_total * 3 // 8
    group_rows = [row_total // 2, row_total // 4, row_total // 4]
    table = pltpu.VMEM((devices, PAIR_MOST, width), BF16)
    mixes = [pltpu.VMEM((token_count, rows), BF16) for rows in group_rows]
    anywhere = pl.BlockSpec(memory_space=pl.ANY)
    return pl.pallas_call(
        kernel,
        out_shape=pltpu.VMEM((token_count, width), BF16),
        in_specs=[anywhere] * 6,
        out_specs=pl.BlockSpec(memory_space=pltpu.VMEM),
        scratch_shapes=[
            pltpu.VMEM((token_count, width), BF16),
            pltpu.VMEM(w_gate.shape[1:], BF16),
            pltpu.VMEM(w_up.shape[1:], BF16),
            pltpu.VMEM(w_down.shape[1:], BF16),
            pltpu.VMEM(chosen.shape, jnp.int32),
            pltpu.VMEM(chosen.shape, F32),
            pltpu.VMEM((row_total, chosen.shape[1]), jnp.int32),
            pltpu.VMEM((row_total, chosen.shape[1]), F32),
            table,
            table,
            table,
            table,
            pltpu.VMEM((pass_rows, width), BF16),
            pltpu.VMEM((pass_rows, hidden_total), BF16),
            pltpu.VMEM((token_count, width), F32),
            mixes,
            mixes,
            pltpu.SemaphoreType.DMA((3,)),
            pltpu.SemaphoreType.DMA((3 * WEIGHT_CUTS,)),
            pltpu.SemaphoreType.DMA((1,)),
            pltpu.SemaphoreType.DMA((4,)),
            pltpu.SemaphoreType.DMA((1,)),
            pltpu.SemaphoreType.DMA((3,)),
        ],
        compiler_params=pltpu.CompilerParams(
            collective_id=0, has_side_effects=True, vmem_limit_bytes=58 * 1024 * 1024
        ),
    )(tokens, w_gate, w_up, w_down, chosen, gate_weights)


def solution(mesh):
    return jax.shard_map(
        shards,
        mesh=mesh,
        in_specs=(
            P(("grp", "loc"), None),
            P(("grp", "loc"), None, None),
            P(("grp", "loc"), None, None),
            P(("grp", "loc"), None, None),
            P(),
            P(),
        ),
        out_specs=P(("grp", "loc"), None),
        check_vma=False,
    )
```

time: 34.7 us -> 32.8 us (0.945)
  the two profiles are of different devices: /device:TPU:0 before, /device:TPU:16 now
where the time goes in v2:
time: 32.8 us; the launch traced here: 32.6 us
  Pallas kernels  31.8 us (97%)
  local copies, waits for them, and re-layouts  0.8 us (2%)
    pallas_call x1, Pallas kernels, shards(): pl.pallas_call(kernel, out_shape=pltpu.VMEM((token_count, width), BF16),...  31.8 us
    unnamed x1, local copies, waits for them, and re-layouts  0.8 us

profile of v2, /device:TPU:16, one launch (start us, length us, event | category | flops | bytes accessed | tf_op | source)
XLA Modules:
  0.0 32.6 jit_solution(6160855325950948911)
XLA Ops:
  0.0 31.8 %shard_map.64 = bf16[256,1024]{1,0:T(8,128)(2,1)S(1)} custom-call(bf16[256,1024]{1,0:T(8,128)(2,1)} %tokens_hbm.1, bf16[1,1024,2816]{2,1,0:T(8,128)(2,1)} %gate_hbm.1, bf16[1,1024,2816]{2,1,0:T(8,128)(2,1)} %up_hbm.1, bf16[1,2816,1024]{2,1,0:T(8,128)(2,1)} %down_hbm.1, s32[32,128]{1,0:T(8,128)} %chosen_hbm.1, f32[32,128]{1,0:T(8,128)} %weight_hbm.1), custom_call_target="tpu_custom_call" | custom-call | tf_op jit(solution)/shard_map/pallas_call | solution.py:263
  31.8 0.8 %copy.8 = bf16[256,1024]{1,0:T(8,128)(2,1)} copy(bf16[256,1024]{1,0:T(8,128)(2,1)S(1)} %shard_map.64) | data formatting | bytes 1048576

commit v3 on v2

--- a/solution.py
+++ b/solution.py
@@ -18,6 +18,16 @@
         if size % tile == 0:
             return tile
     return size
+
+
+def cuts(block):
+    early = block * 3 // 8
+    return early, block - early
+
+
+def group_sizes(block):
+    early, late = cuts(block)
+    return [2 * block, 2 * early, 2 * late]
 
 
 def flip(value, mask):
@@ -70,7 +80,7 @@
     side = plane // 2
     outer = (side + plane % 2 + 1) % 2
     block = quarter * group_count
-    part = block // 2
+    early, late = cuts(block)
 
     def partner(plane_there, turn):
         return (
@@ -85,22 +95,26 @@
         return other * block + turn
 
     def far_out(sub, kind, turn):
-        return (2 + sub) * block + kind * part + turn
+        if sub:
+            return 2 * block + 2 * early + kind * late + turn
+        return 2 * block + kind * early + turn
 
     def near_in(other, turn):
-        return other * (block + part) + turn
+        return other * (block + early) + turn
 
     def far_in(sub, kind, turn):
-        return turn + (7 * part - kind * part if sub else block + kind * (block + part))
+        if sub:
+            return 2 * (block + early) + (1 - kind) * late + turn
+        return block + kind * (block + early) + turn
 
     def far_pass(sub, kind):
         return 3 - kind if sub else kind
 
     dispatch, results = [], [[], [], [], []]
-    for sub in range(2):
-        for turn in range(part):
+    for sub, count in enumerate((early, late)):
+        for turn in range(count):
             for kind in range(2):
-                peer = partner(far_plane(kind), sub * part + turn)
+                peer = partner(far_plane(kind), sub * early + turn)
                 there, number = far_in(sub, outer, turn), far_pass(sub, outer)
                 dispatch.append((far_out(sub, kind, turn), peer, there, number))
                 home = far_out(sub, outer, turn)
@@ -112,10 +126,10 @@
             near.append((near_out(other, turn), peer, near_in(other, turn), other))
             results[other].append((near_in(other, turn), peer, near_out(other, turn), 0))
     dispatch = near + dispatch
-    passes = [
-        (0, block + part), (block + part, block + part), (6 * part, part), (7 * part, part)
-    ]
-    groups = [(0, 2 * block), (2 * block, block), (3 * block, block)]
+    counts = [block + early, block + early, late, late]
+    passes = [(sum(counts[:number]), count) for number, count in enumerate(counts)]
+    counts = group_sizes(block)
+    groups = [(sum(counts[:number]), count) for number, count in enumerate(counts)]
     barrier = pltpu.get_barrier_semaphore()
     for at, peer, _, _ in reversed(dispatch):
         if at:
@@ -255,8 +269,9 @@
     token_count, width = tokens.shape
     hidden_total = w_gate.shape[2]
     row_total = devices * PAIR_MOST
-    pass_rows = row_total * 3 // 8
-    group_rows = [row_total // 2, row_total // 4, row_total // 4]
+    block = devices // 4
+    pass_rows = (block + max(cuts(block))) * PAIR_MOST
+    group_rows = [count * PAIR_MOST for count in group_sizes(block)]
     table = pltpu.VMEM((devices, PAIR_MOST, width), BF16)
     mixes = [pltpu.VMEM((token_count, rows), BF16) for rows in group_rows]
     anywhere = pl.BlockSpec(memory_space=pl.ANY)

time: 32.8 us -> 31.6 us (0.963)
  the two profiles are of different devices: /device:TPU:16 before, /device:TPU:8 now
where the time goes in v3:
time: 31.6 us; the launch traced here: 31.4 us
  Pallas kernels  30.6 us (97%)
  local copies, waits for them, and re-layouts  0.8 us (3%)
    pallas_call x1, Pallas kernels, shards(): pl.pallas_call(kernel, out_shape=pltpu.VMEM((token_count, width), BF16),...  30.6 us
    unnamed x1, local copies, waits for them, and re-layouts  0.8 us

profile of v3, /device:TPU:8, one launch (start us, length us, event | category | flops | bytes accessed | tf_op | source)
XLA Modules:
  0.0 31.4 jit_solution(11152302056645064034)
XLA Ops:
  0.0 30.6 %shard_map.64 = bf16[256,1024]{1,0:T(8,128)(2,1)S(1)} custom-call(bf16[256,1024]{1,0:T(8,128)(2,1)} %tokens_hbm.1, bf16[1,1024,2816]{2,1,0:T(8,128)(2,1)} %gate_hbm.1, bf16[1,1024,2816]{2,1,0:T(8,128)(2,1)} %up_hbm.1, bf16[1,2816,1024]{2,1,0:T(8,128)(2,1)} %down_hbm.1, s32[32,128]{1,0:T(8,128)} %chosen_hbm.1, f32[32,128]{1,0:T(8,128)} %weight_hbm.1), custom_call_target="tpu_custom_call" | custom-call | tf_op jit(solution)/shard_map/pallas_call | solution.py:278
  30.6 0.8 %copy.8 = bf16[256,1024]{1,0:T(8,128)(2,1)} copy(bf16[256,1024]{1,0:T(8,128)(2,1)S(1)} %shard_map.64) | data formatting | bytes 1048576

commit v4 on v3

--- a/solution.py
+++ b/solution.py
@@ -62,14 +62,14 @@
     gathered,
     hidden,
     total,
-    mix_hi,
-    mix_lo,
+    mix,
     small_sem,
     load_sem,
     send_sem,
     recv_sem,
     return_send_sem,
     return_sem,
+    entered,
 ):
     group_count, local_count = lax.axis_size("grp"), lax.axis_size("loc")
     devices = group_count * local_count
@@ -110,30 +110,40 @@
     def far_pass(sub, kind):
         return 3 - kind if sub else kind
 
-    dispatch, results = [], [[], [], [], []]
+    far, results = {}, [[], [], [], []]
     for sub, count in enumerate((early, late)):
         for turn in range(count):
             for kind in range(2):
                 peer = partner(far_plane(kind), sub * early + turn)
                 there, number = far_in(sub, outer, turn), far_pass(sub, outer)
-                dispatch.append((far_out(sub, kind, turn), peer, there, number))
+                entry = (far_out(sub, kind, turn), peer, there, number)
+                far.setdefault((sub, kind), []).append(entry)
                 home = far_out(sub, outer, turn)
                 results[far_pass(sub, kind)].append((far_in(sub, kind, turn), peer, home, 1 + sub))
-    near = []
+    near = [[], []]
     for other in (1, 0):
         for turn in range(block):
             peer = partner(flip(plane, other), turn)
-            near.append((near_out(other, turn), peer, near_in(other, turn), other))
+            near[other].append((near_out(other, turn), peer, near_in(other, turn), other))
             results[other].append((near_in(other, turn), peer, near_out(other, turn), 0))
-    dispatch = near + dispatch
+    mixed = [entry for sub in range(2) for pair in zip(far[sub, 0], far[sub, 1]) for entry in pair]
+    dispatch = near[1] + near[0] + mixed
     counts = [block + early, block + early, late, late]
     passes = [(sum(counts[:number]), count) for number, count in enumerate(counts)]
     counts = group_sizes(block)
     groups = [(sum(counts[:number]), count) for number, count in enumerate(counts)]
     barrier = pltpu.get_barrier_semaphore()
-    for at, peer, _, _ in reversed(dispatch):
-        if at:
-            pl.semaphore_signal(barrier, inc=1, device_id=peer, device_id_type=MESH)
+
+    def signal(semaphore, peer):
+        pl.semaphore_signal(semaphore, inc=1, device_id=peer, device_id_type=MESH)
+
+    @pl.when(plane != 3)
+    def _():
+        for _, peer, _, _ in reversed(near[1]):
+            signal(barrier, peer)
+
+    for _, peer, _, _ in reversed(near[0][1:] + mixed):
+        signal(barrier, peer)
     small = [
         pltpu.make_async_copy(chosen_hbm, chosen, small_sem.at[0]),
         pltpu.make_async_copy(weight_hbm, weights, small_sem.at[1]),
@@ -186,7 +196,12 @@
             loads.append(copy)
     picked = jnp.dot(select_table, tokens[...], preferred_element_type=F32)
     outgoing[...] = picked.reshape(devices, PAIR_MOST, width).astype(BF16)
-    pl.semaphore_wait(barrier, devices - 1)
+    pl.semaphore_wait(barrier, devices - 1 - block * (plane // 2 * (3 - plane)))
+
+    @pl.when(plane == 3)
+    def _():
+        for _, peer, _, _ in near[1]:
+            signal(entered, peer)
 
     def send(source, place, send_sems, sems, entry):
         at, peer, mirror, sem = entry
@@ -206,16 +221,25 @@
         view = place.at[pl.ds(first, count)]
         pltpu.make_async_copy(view, view, sem).wait()
 
-    for entry in dispatch:
-        send(outgoing, received, send_sem, recv_sem, entry)
+    @pl.when(plane == 2)
+    def _():
+        for entry in mixed + near[0]:
+            send(outgoing, received, send_sem, recv_sem, entry)
+        pl.semaphore_wait(entered, block)
+        for entry in near[1]:
+            send(outgoing, received, send_sem, recv_sem, entry)
+
+    @pl.when(plane != 2)
+    def _():
+        for entry in dispatch:
+            send(outgoing, received, send_sem, recv_sem, entry)
     mixing = jnp.where(select, pick_weight, 0.0).T
     high = mixing.astype(BF16)
     low = (mixing - high.astype(F32)).astype(BF16)
     for number, (first, count) in enumerate(groups):
         rows = slice(first * PAIR_MOST, (first + count) * PAIR_MOST)
-        mix_hi[number][...] = high[:, rows]
-        mix_lo[number][...] = low[:, rows]
-    for copy in loads:
+        mix[number][...] = jnp.concatenate([high[:, rows], low[:, rows]], axis=1)
+    for copy in loads[: 2 * WEIGHT_CUTS]:
         copy.wait()
 
     hidden_total = w_gate.shape[1]
@@ -234,6 +258,9 @@
             return carry
 
         lax.fori_loop(0, hidden_total // hidden_tile, expand, 0, unroll=True)
+        if not number:
+            for copy in loads[2 * WEIGHT_CUTS :]:
+                copy.wait()
 
         def contract(tile, carry, rows=rows, first=first, count=count):
             columns = pl.ds(pl.multiple_of(tile * width_tile, width_tile), width_tile)
@@ -244,15 +271,36 @@
             return carry
 
         lax.fori_loop(0, width // width_tile, contract, 0, unroll=True)
-        for entry in results[number]:
-            send(produced, back, return_send_sem, return_sem, entry)
+        if number < 2:
+
+            @pl.when(side == 1 - number)
+            def _():
+                for entry in results[0]:
+                    send(produced, back, return_send_sem, return_sem, entry)
+
+        if number == 3:
+            high = grp // (group_count // 2)
+            middle = late * 3 // 5
+
+            @pl.when(high == 0)
+            def _():
+                for entry in results[3]:
+                    send(produced, back, return_send_sem, return_sem, entry)
+
+            @pl.when(high == 1)
+            def _():
+                for entry in results[3][middle:] + results[3][:middle]:
+                    send(produced, back, return_send_sem, return_sem, entry)
+        elif number:
+            for entry in results[number]:
+                send(produced, back, return_send_sem, return_sem, entry)
 
     for number, (first, count) in enumerate(groups):
         rows = count * PAIR_MOST
         wait_blocks(back, return_sem.at[number], first, count)
         returned = back[pl.ds(first, count)].astype(F32).reshape(rows, width).astype(BF16)
-        result = jnp.dot(mix_hi[number][...], returned, preferred_element_type=F32)
-        result += jnp.dot(mix_lo[number][...], returned, preferred_element_type=F32)
+        twice = jnp.concatenate([returned, returned], axis=0)
+        result = jnp.dot(mix[number][...], twice, preferred_element_type=F32)
         if number:
             result += total[...]
         if number == len(groups) - 1:
@@ -273,7 +321,7 @@
     pass_rows = (block + max(cuts(block))) * PAIR_MOST
     group_rows = [count * PAIR_MOST for count in group_sizes(block)]
     table = pltpu.VMEM((devices, PAIR_MOST, width), BF16)
-    mixes = [pltpu.VMEM((token_count, rows), BF16) for rows in group_rows]
+    mixes = [pltpu.VMEM((token_count, 2 * rows), BF16) for rows in group_rows]
     anywhere = pl.BlockSpec(memory_space=pl.ANY)
     return pl.pallas_call(
         kernel,
@@ -297,13 +345,13 @@
             pltpu.VMEM((pass_rows, hidden_total), BF16),
             pltpu.VMEM((token_count, width), F32),
             mixes,
-            mixes,
             pltpu.SemaphoreType.DMA((3,)),
             pltpu.SemaphoreType.DMA((3 * WEIGHT_CUTS,)),
             pltpu.SemaphoreType.DMA((1,)),
             pltpu.SemaphoreType.DMA((4,)),
             pltpu.SemaphoreType.DMA((1,)),
             pltpu.SemaphoreType.DMA((3,)),
+            pltpu.SemaphoreType.REGULAR,
         ],
         compiler_params=pltpu.CompilerParams(
             collective_id=0, has_side_effects=True, vmem_limit_bytes=58 * 1024 * 1024

time: 31.6 us -> 30.2 us (0.956)
  the two profiles are of different devices: /device:TPU:8 before, /device:TPU:13 now
where the time goes in v4:
time: 30.2 us; the launch traced here: 30 us
  Pallas kernels  29.2 us (97%)
  local copies, waits for them, and re-layouts  0.8 us (3%)
    pallas_call x1, Pallas kernels, shards(): pl.pallas_call(kernel, out_shape=pltpu.VMEM((token_count, width), BF16),...  29.2 us
    unnamed x1, local copies, waits for them, and re-layouts  0.8 us

profile of v4, /device:TPU:13, one launch (start us, length us, event | category | flops | bytes accessed | tf_op | source)
XLA Modules:
  0.0 30.0 jit_solution(849527342420860600)
XLA Ops:
  0.0 29.2 %shard_map.64 = bf16[256,1024]{1,0:T(8,128)(2,1)S(1)} custom-call(bf16[256,1024]{1,0:T(8,128)(2,1)} %tokens_hbm.1, bf16[1,1024,2816]{2,1,0:T(8,128)(2,1)} %gate_hbm.1, bf16[1,1024,2816]{2,1,0:T(8,128)(2,1)} %up_hbm.1, bf16[1,2816,1024]{2,1,0:T(8,128)(2,1)} %down_hbm.1, s32[32,128]{1,0:T(8,128)} %chosen_hbm.1, f32[32,128]{1,0:T(8,128)} %weight_hbm.1), custom_call_target="tpu_custom_call" | custom-call | tf_op jit(solution)/shard_map/pallas_call | solution.py:326
  29.2 0.8 %copy.8 = bf16[256,1024]{1,0:T(8,128)(2,1)} copy(bf16[256,1024]{1,0:T(8,128)(2,1)S(1)} %shard_map.64) | data formatting | bytes 1048576

commit v5 on v4

--- a/solution.py
+++ b/solution.py
@@ -239,22 +239,26 @@
     for number, (first, count) in enumerate(groups):
         rows = slice(first * PAIR_MOST, (first + count) * PAIR_MOST)
         mix[number][...] = jnp.concatenate([high[:, rows], low[:, rows]], axis=1)
+    filled = passes[0][1] * PAIR_MOST
+    if filled < gathered.shape[0]:
+        gathered[filled:, :] = jnp.zeros_like(gathered[filled:, :])
     for copy in loads[: 2 * WEIGHT_CUTS]:
         copy.wait()
 
     hidden_total = w_gate.shape[1]
     hidden_tile, width_tile = tile_of(hidden_total), tile_of(width)
+    full = gathered.shape[0]
     for number, (first, count) in enumerate(passes):
         rows = count * PAIR_MOST
         wait_blocks(received, recv_sem.at[number], first, count)
         arrived = received[pl.ds(first, count)].astype(F32)
         gathered[:rows, :] = arrived.reshape(rows, width).astype(BF16)
 
-        def expand(tile, carry, rows=rows):
+        def expand(tile, carry):
             columns = pl.ds(pl.multiple_of(tile * hidden_tile, hidden_tile), hidden_tile)
-            gate_pre = jnp.dot(gathered[:rows, :], w_gate[:, columns], preferred_element_type=F32)
-            up_pre = jnp.dot(gathered[:rows, :], w_up[:, columns], preferred_element_type=F32)
-            hidden[:rows, columns] = (gate_pre / (1.0 + jnp.exp(-gate_pre)) * up_pre).astype(BF16)
+            gate_pre = jnp.dot(gathered[:full, :], w_gate[:, columns], preferred_element_type=F32)
+            up_pre = jnp.dot(gathered[:full, :], w_up[:, columns], preferred_element_type=F32)
+            hidden[:full, columns] = (gate_pre / (1.0 + jnp.exp(-gate_pre)) * up_pre).astype(BF16)
             return carry
 
         lax.fori_loop(0, hidden_total // hidden_tile, expand, 0, unroll=True)
@@ -264,8 +268,8 @@
 
         def contract(tile, carry, rows=rows, first=first, count=count):
             columns = pl.ds(pl.multiple_of(tile * width_tile, width_tile), width_tile)
-            result = jnp.dot(hidden[:rows, :], w_down[:, columns], preferred_element_type=F32)
-            produced[pl.ds(first, count), :, columns] = result.reshape(
+            result = jnp.dot(hidden[:full, :], w_down[:, columns], preferred_element_type=F32)
+            produced[pl.ds(first, count), :, columns] = result[:rows].reshape(
                 count, PAIR_MOST, width_tile
             ).astype(BF16)
             return carry
@@ -318,7 +322,7 @@
     hidden_total = w_gate.shape[2]
     row_total = devices * PAIR_MOST
     block = devices // 4
-    pass_rows = (block + max(cuts(block))) * PAIR_MOST
+    pass_rows = -(-(block + max(cuts(block))) * PAIR_MOST // 32) * 32
     group_rows = [count * PAIR_MOST for count in group_sizes(block)]
     table = pltpu.VMEM((devices, PAIR_MOST, width), BF16)
     mixes = [pltpu.VMEM((token_count, 2 * rows), BF16) for rows in group_rows]

time: 30.2 us -> 30 us (level)
  the two profiles are of different devices: /device:TPU:13 before, /device:TPU:21 now
where the time goes in v5:
time: 30 us; the launch traced here: 29.8 us
  Pallas kernels  29 us (97%)
  local copies, waits for them, and re-layouts  0.8 us (3%)
    pallas_call x1, Pallas kernels, shards(): pl.pallas_call(kernel, out_shape=pltpu.VMEM((token_count, width), BF16),...  29 us
    unnamed x1, local copies, waits for them, and re-layouts  0.8 us

profile of v5, /device:TPU:21, one launch (start us, length us, event | category | flops | bytes accessed | tf_op | source)
XLA Modules:
  0.0 29.8 jit_solution(14967072760489484182)
XLA Ops:
  0.0 29.0 %shard_map.64 = bf16[256,1024]{1,0:T(8,128)(2,1)S(1)} custom-call(bf16[256,1024]{1,0:T(8,128)(2,1)} %tokens_hbm.1, bf16[1,1024,2816]{2,1,0:T(8,128)(2,1)} %gate_hbm.1, bf16[1,1024,2816]{2,1,0:T(8,128)(2,1)} %up_hbm.1, bf16[1,2816,1024]{2,1,0:T(8,128)(2,1)} %down_hbm.1, s32[32,128]{1,0:T(8,128)} %chosen_hbm.1, f32[32,128]{1,0:T(8,128)} %weight_hbm.1), custom_call_target="tpu_custom_call" | custom-call | tf_op jit(solution)/shard_map/pallas_call | solution.py:330
  29.0 0.8 %copy.8 = bf16[256,1024]{1,0:T(8,128)(2,1)} copy(bf16[256,1024]{1,0:T(8,128)(2,1)S(1)} %shard_map.64) | data formatting | bytes 1048576
